TPU v7x, 32 devices: a whole 2x2x4 slice. The times are simulated.
32 devices in a mesh: group: 4 (over x, core), seq: 2 (over y), expert: 4 (over z).
Axes of the slice: x: 2, y: 2, z: 4, core: 2. Of those that a mesh axis runs over, the one named last changes fastest.
Arguments:
- queries: bfloat16 [16, 32, 128], P('expert', 'group')
- keys: bfloat16 [16, 256, 8, 128], P('expert', 'seq', 'group')
- values: bfloat16 [16, 256, 8, 128], P('expert', 'seq', 'group'), may hold values from -48 to 48
- block_of_slot: int32 [16, 16], P('expert', 'seq'), may hold values from 0 to 15, each once within a row
- lengths: int32 [16], P('expert'), may hold values from 128 to 256
- out_proj: bfloat16 [4096, 4096], P('group', 'seq'), may hold values from -0.09375 to 0.09375
- residual: bfloat16 [16, 4096], P('expert', 'seq'), may hold values from -6 to 6
- norm_gain: bfloat16 [4096], replicated, may hold values from 0.25 to 1.75
- router: bfloat16 [4096, 8], replicated, may hold values from -0.09375 to 0.09375
- routes: int32 [16, 2], P('expert'), may hold values from 0 to 7, all different within a row; in each aligned block of 4 rows (0 to 3, 4 to 7, ...) at most 2 rows name the same one
- w_gate: bfloat16 [8, 4096, 14336], P('expert', None, ('group', 'seq')), may hold values from -0.09375 to 0.09375
- w_up: bfloat16 [8, 4096, 14336], P('expert', None, ('group', 'seq')), may hold values from -0.09375 to 0.09375
- w_down: bfloat16 [8, 14336, 4096], P('expert', ('group', 'seq')), may hold values from -0.046875 to 0.046875
Outputs:
- layer_out: bfloat16 [16, 4096], P('expert', 'seq')
Inputs may be any that keep to these rules, and one draw needn't show every extreme that they name: `block_of_slot`: each row lists every logical block once. `routes`: the two ids of a row differ; among the 4 rows of one device no expert is named more than 2 times, and in some such blocks one expert is named exactly 2 times.
All inputs are finite; a program needn't handle non-finite values.
Results may differ from a plain program's by a relative error of at most 0.013.
Values may be sent and summed in bfloat16 or wider, within the bound.
No kernel may reach another device: no remote copies, remote signals or barrier semaphores. Data moves between devices by JAX's collectives and lax.ppermute only.
A program may use at most 128 MiB of HBM per device.

v0:
```python
import jax
import jax.numpy as jnp
from jax import lax
from jax.sharding import PartitionSpec as P

BLOCK = 16
CAPACITY = 2
masked_score = -1e30


def combined_all(value, axis, combine):
    everything = jax.tree.map(lambda part: lax.all_gather(part, axis), value)
    initial = jax.tree.map(lambda part: part[0], everything)

    def hop(k, so_far):
        return combine(so_far, jax.tree.map(lambda part: part[k], everything))

    return lax.fori_loop(1, lax.axis_size(axis), hop, initial)


def combine_carry(earlier, later):
    high_a, total_a, sums_a = earlier
    high_b, total_b, sums_b = later
    highest = jnp.maximum(high_a, high_b)
    scale_a = jnp.exp(high_a - highest)
    scale_b = jnp.exp(high_b - highest)
    return (
        highest,
        total_a * scale_a + total_b * scale_b,
        sums_a * scale_a[..., None] + sums_b * scale_b[..., None],
    )


def shards(
    queries,
    keys,
    values,
    block_of_slot,
    lengths,
    out_proj,
    residual,
    norm_gain,
    router,
    routes,
    w_gate,
    w_up,
    w_down,
):
    batch_rows, local_heads, head_dim = queries.shape
    span_len = keys.shape[1]
    kv_local = keys.shape[2]
    per_kv = local_heads // kv_local
    grouped = queries.reshape(batch_rows, kv_local, per_kv, head_dim)
    scores = jnp.einsum(
        "rkgd,rlkd->rkgl", grouped, keys, preferred_element_type=jnp.float32
    ) * head_dim ** (-0.5)
    offsets = jnp.arange(BLOCK, dtype=jnp.int32)
    position = (block_of_slot[:, :, None] * BLOCK + offsets[None, None, :]).reshape(
        batch_rows, span_len
    )
    visible = (position < lengths[:, None])[:, None, None, :]
    masked = jnp.where(visible, scores, masked_score)
    highest = jnp.max(masked, axis=-1)
    probs = jnp.where(visible, jnp.exp(masked - highest[..., None]), 0.0)
    totals = jnp.sum(probs, axis=-1)
    weighted = jnp.einsum(
        "rkgl,rlkd->rkgd", probs.astype(jnp.bfloat16), values, preferred_element_type=jnp.float32
    )
    local_carry = (highest, totals, weighted)
    highest, totals, weighted = combined_all(local_carry, "seq", combine_carry)
    attended = (
        (weighted / totals[..., None])
        .astype(jnp.bfloat16)
        .reshape(batch_rows, local_heads * head_dim)
    )
    partial_value = jnp.dot(attended, out_proj, preferred_element_type=jnp.float32)
    attention = lax.psum(partial_value, "group")
    hidden = residual.astype(jnp.float32) + attention
    full_rows = lax.all_gather(hidden, "seq", axis=1, tiled=True)
    meansq = jnp.mean(full_rows * full_rows, axis=-1, keepdims=True)
    normed = (full_rows * lax.rsqrt(meansq + 1e-05) * norm_gain.astype(jnp.float32)).astype(
        jnp.bfloat16
    )
    logits = jnp.dot(normed, router, preferred_element_type=jnp.float32)
    experts = router.shape[1]
    onehot = (routes[:, :, None] == jnp.arange(experts, dtype=jnp.int32)[None, None, :]).astype(
        jnp.int32
    )
    chosen = jnp.sum(onehot.astype(jnp.float32) * logits[:, None, :], axis=-1)
    gate_probs = jax.nn.softmax(chosen, axis=-1)
    per_row = jnp.sum(onehot, axis=1)
    earlier = jnp.cumsum(per_row, axis=0) - per_row
    slot_index = jnp.sum(onehot * earlier[:, None, :], axis=2)
    in_slot = (
        slot_index[:, :, None] == jnp.arange(CAPACITY, dtype=jnp.int32)[None, None, :]
    ).astype(jnp.int32)
    chart = onehot[:, :, :, None] * in_slot[:, :, None, :]
    picker = jnp.sum(chart, axis=1).astype(jnp.bfloat16)
    outbound = jnp.einsum("rec,rd->ecd", picker, normed, preferred_element_type=jnp.float32).astype(
        jnp.bfloat16
    )
    expert_devs = lax.axis_size("expert")
    local_experts = experts // expert_devs
    model_width = normed.shape[1]
    outbound = outbound.reshape(expert_devs, local_experts, CAPACITY, model_width)
    inbound = lax.all_to_all(outbound, "expert", split_axis=0, concat_axis=0, tiled=True)
    gate_act = jnp.einsum("secd,edf->secf", inbound, w_gate, preferred_element_type=jnp.float32)
    upper = jnp.einsum("secd,edf->secf", inbound, w_up, preferred_element_type=jnp.float32)
    activated = (jax.nn.silu(gate_act) * upper).astype(jnp.bfloat16)
    down_terms = jnp.einsum("secf,efd->secd", activated, w_down, preferred_element_type=jnp.float32)
    summed = lax.psum(down_terms.astype(jnp.bfloat16), ("group", "seq")).astype(jnp.float32)
    col_width = summed.shape[3] // lax.axis_size("seq")
    my_cols = lax.dynamic_slice_in_dim(summed, lax.axis_index("seq") * col_width, col_width, 3)
    returned = lax.all_to_all(
        my_cols.astype(jnp.bfloat16), "expert", split_axis=0, concat_axis=0, tiled=True
    )
    returned = returned.reshape(experts, CAPACITY, returned.shape[3]).astype(jnp.float32)
    mixing = jnp.sum(gate_probs[:, :, None, None] * chart.astype(jnp.float32), axis=1)
    expert_mix = jnp.einsum("rec,ecd->rd", mixing, returned, precision=lax.Precision.HIGHEST)
    return (hidden + expert_mix).astype(jnp.bfloat16)


def solution(mesh):
    return jax.shard_map(
        shards,
        mesh=mesh,
        in_specs=(
            P("expert", "group", None),
            P("expert", "seq", "group", None),
            P("expert", "seq", "group", None),
            P("expert", "seq"),
            P("expert"),
            P("group", "seq"),
            P("expert", "seq"),
            P(),
            P(),
            P("expert", None),
            P("expert", None, ("group", "seq")),
            P("expert", None, ("group", "seq")),
            P("expert", ("group", "seq"), None),
        ),
        out_specs=P("expert", "seq"),
        check_vma=False,
    )
```

profile of v0, /device:TPU:0, one launch (start us, length us, event | category | flops | bytes accessed | tf_op | source)
XLA Modules:
  0.0 164.8 jit_solution(3506737250032493510)
XLA Ops:
  6.5 0.8 fusion.56
  7.3 0.7 fusion.55
  8.1 0.7 broadcast_multiply_fusion
  9.0 0.7 add_compare_fusion
  9.8 1.0 fusion.64
  10.8 5.3 %all-gather.1 = f32[8,2,4]{2,1,0:T(2,128)S(1)} all-gather(f32[4,2,4]{2,1,0:T(2,128)S(1)} %get-tuple-element.22), channel_id=3, replica_groups=mesh['group'=4,'seq'=2,'expert'=4] {'seq'}, dimensions={0}, use_global_device_ids=true | all-gather | bytes 384 | tf_op jit(solution)/shard_map/all_gather | solution.py:12
  16.1 0.2 fusion.44
  16.3 1.2 fusion.29
  17.4 4.4 %all-gather = f32[8,2,4,128]{3,2,1,0:T(4,128)S(1)} all-gather(f32[4,2,4,128]{3,2,1,0:T(4,128)S(1)} %fusion.29), channel_id=2, replica_groups=mesh['group'=4,'seq'=2,'expert'=4] {'seq'}, dimensions={0}, use_global_device_ids=true | all-gather | bytes 49152 | tf_op jit(solution)/shard_map/all_gather | solution.py:12
  21.8 4.3 %all-gather.2 = f32[8,2,4]{2,1,0:T(2,128)S(1)} all-gather(f32[4,2,4]{2,1,0:T(2,128)S(1)} %fusion.44), channel_id=4, replica_groups=mesh['group'=4,'seq'=2,'expert'=4] {'seq'}, dimensions={0}, use_global_device_ids=true | all-gather | bytes 384 | tf_op jit(solution)/shard_map/all_gather | solution.py:12
  26.2 0.1 fusion.43
  26.3 2.8 %fusion.65 = f32[4,2048]{1,0:T(4,128)S(1)} fusion(bf16[4,1024]{1,0:T(4,128)(2,1)S(1)} %reshape.183, bf16[1024,2048]{1,0:T(8,128)(2,1)} %param.18), kind=kOutput, calls=%fused_computation.72 | convolution fusion | flops 16777216 | bytes 4235264 | tf_op jit(solution)/shard_map/dot_general | solution.py:76
  29.2 10.3 %psum.14 = f32[4,2048]{1,0:T(4,128)S(1)} all-reduce(f32[4,2048]{1,0:T(4,128)S(1)} %fusion.65), channel_id=1, replica_groups=mesh['group'=4,'seq'=2,'expert'=4] {'group'}, use_global_device_ids=true, to_apply=%region_2.3 | all-reduce | flops 8192 | bytes 65536 | tf_op jit(solution)/shard_map/psum | solution.py:77
  39.5 0.9 select_reduce_fusion
  40.4 0.7 convert_add_fusion
  41.1 4.6 %all_gather.27 = f32[4,4096]{1,0:T(4,128)S(1)} all-gather(f32[4,2048]{1,0:T(4,128)S(1)} %convert_add_fusion), channel_id=1, replica_groups=mesh['group'=4,'seq'=2,'expert'=4] {'seq'}, dimensions={1}, use_global_device_ids=true | all-gather | bytes 98304 | tf_op jit(solution)/shard_map/all_gather | solution.py:79
  45.7 0.7 convert_element_type.66
  46.4 0.1 multiply_reduce_fusion
  46.7 0.2 convolution_convert_fusion
  47.0 0.8 copy.42
  47.7 5.4 %all-to-all-start = ((bf16[4,2,2,4096]{3,2,1,0:T(2,128)(2,1)}), bf16[4,2,2,4096]{3,2,1,0:T(2,128)(2,1)S(1)}, u32[]{:S(2)}, u32[]{:S(2)}) async-start(bf16[4,2,2,4096]{3,2,1,0:T(2,128)(2,1)} %bitcast.2), calls=%async_computation | async-start | bytes 262144 | tf_op jit(solution)/shard_map/all_to_all | solution.py:106
  53.1 1.0 fusion.66
  54.1 0.9 multiply_reduce_fusion.2
  55.0 4.0 %all-to-all-done = bf16[4,2,2,4096]{3,2,1,0:T(2,128)(2,1)S(1)} async-done(((bf16[4,2,2,4096]{3,2,1,0:T(2,128)(2,1)}), bf16[4,2,2,4096]{3,2,1,0:T(2,128)(2,1)S(1)}, u32[]{:S(2)}, u32[]{:S(2)}) %all-to-all-start) | async-done | bytes 131104 | tf_op jit(solution)/shard_map/all_to_all | solution.py:106
  59.1 11.6 %fusion.12 = f32[4,2,2,1792]{3,0,2,1:T(4,128)S(1)} fusion(bf16[2,4096,1792]{2,1,0:T(8,128)(2,1)} %param.23, bf16[4,2,2,4096]{3,2,1,0:T(2,128)(2,1)S(1)} %all-to-all-done), kind=kOutput, calls=%fused_computation.9 | convolution fusion | flops 234881024 | bytes 29605888 | tf_op jit(solution)/shard_map/secd,edf->secf/dot_general | solution.py:107
  70.6 21.8 %fusion.9 = bf16[4,2,2,4096]{3,0,2,1:T(4,128)(2,1)} fusion(bf16[2,1792,4096]{2,1,0:T(8,128)(2,1)} %param.25, bf16[2,4096,1792]{2,1,0:T(8,128)(2,1)} %param.24, f32[4,2,2,1792]{3,0,2,1:T(4,128)S(1)} %fusion.12, bf16[4,2,2,4096]{3,2,1,0:T(2,128)(2,1)S(1)} %all-to-all-done), kind=kOutput, calls=%fused_computation.8 | convolution fusion | flops 469999616 | bytes 59097088 | tf_op jit(solution)/shard_map/secf,efd->secd/dot_general | solution.py:110
  92.5 52.7 %all-reduce.2.cloned.1.call-done = bf16[4,2,2,4096]{3,0,2,1:T(4,128)(2,1)} async-done(((bf16[4,2,2,4096]{3,0,2,1:T(4,128)(2,1)}), bf16[4,2,2,4096]{3,0,2,1:T(4,128)(2,1)}) %all-reduce.2.cloned.1.call-update) | async-done | bytes 131088 | tf_op jit(solution)/shard_map/psum | solution.py:111
  145.2 0.9 convert_convert_fusion
  146.1 0.7 copy.37
  146.8 4.6 %all-to-all-start.1 = ((bf16[4,2,2,2048]{3,2,1,0:T(2,128)(2,1)}), bf16[4,2,2,2048]{3,2,1,0:T(2,128)(2,1)S(1)}, u32[]{:S(2)}, u32[]{:S(2)}) async-start(bf16[4,2,2,2048]{3,2,1,0:T(2,128)(2,1)} %copy.37), calls=%async_computation.1 | async-start | bytes 131072 | tf_op jit(solution)/shard_map/all_to_all | solution.py:114
  151.5 5.7 %all-to-all-done.1 = bf16[4,2,2,2048]{3,2,1,0:T(2,128)(2,1)S(1)} async-done(((bf16[4,2,2,2048]{3,2,1,0:T(2,128)(2,1)}), bf16[4,2,2,2048]{3,2,1,0:T(2,128)(2,1)S(1)}, u32[]{:S(2)}, u32[]{:S(2)}) %all-to-all-start.1) | async-done | bytes 65568 | tf_op jit(solution)/shard_map/all_to_all | solution.py:114
  157.1 0.8 fusion.27
  (20 shorter events, 0.7 us)
Async XLA Ops:
  6.5 3.2 %copy-start = (bf16[4,128,2,128]{3,2,1,0:T(2,128)(2,1)S(1)}, bf16[4,128,2,128]{3,2,1,0:T(2,128)(2,1)}, u32[]{:S(2)}) copy-start(bf16[4,128,2,128]{3,2,1,0:T(2,128)(2,1)} %param.14) | copy-start | bytes 786436
  47.7 11.3 %all-to-all-start = ((bf16[4,2,2,4096]{3,2,1,0:T(2,128)(2,1)}), bf16[4,2,2,4096]{3,2,1,0:T(2,128)(2,1)S(1)}, u32[]{:S(2)}, u32[]{:S(2)}) async-start(bf16[4,2,2,4096]{3,2,1,0:T(2,128)(2,1)} %bitcast.2), calls=%async_computation | async-start | bytes 262144 | tf_op jit(solution)/shard_map/all_to_all | solution.py:106
  53.1 92.1 %all-reduce.2.cloned.1.call-start = ((), (), s32[]{:S(2)}) async-start(), calls=%async_computation.2 | async-start | bytes 262144 | tf_op jit(solution)/shard_map/psum | solution.py:111
  146.8 10.3 %all-to-all-start.1 = ((bf16[4,2,2,2048]{3,2,1,0:T(2,128)(2,1)}), bf16[4,2,2,2048]{3,2,1,0:T(2,128)(2,1)S(1)}, u32[]{:S(2)}, u32[]{:S(2)}) async-start(bf16[4,2,2,2048]{3,2,1,0:T(2,128)(2,1)} %copy.37), calls=%async_computation.1 | async-start | bytes 131072 | tf_op jit(solution)/shard_map/all_to_all | solution.py:114
Sparse Core Ops, SparseCore 0:
  92.6 52.6 all-reduce.1
where the time goes:
time: 166 us; the launch traced here: 165 us
  waiting for transfers between devices  62.5 us (38%)
  matrix products  40.5 us (24%)
  blocking collectives  28.9 us (17%)
  between operations  13.5 us (8%)
  starting transfers between devices  9.99 us (6%)
  other arithmetic  7.8 us (5%)
  local copies, waits for them, and re-layouts  1.72 us (1%)
    psum x1, waiting for transfers between devices, shards(): lax.psum(down_terms.astype(jnp.bfloat16), ('group', 'seq'))  52.7 us
    dot_general x1, matrix products, shards(): jnp.einsum('secf,efd->secd', activated, w_down, preferred_element_type=jn...  21.8 us
    all_gather x3, blocking collectives, combined_all(): everything = jax.tree.map(lambda part: lax.all_gather(part, axis), value)  14.1 us
    dot_general x1, matrix products, shards(): jnp.einsum('secd,edf->secf', inbound, w_gate, preferred_element_type=jnp....  11.6 us
    psum x1, blocking collectives, shards(): attention = lax.psum(partial_value, 'group')  10.3 us
    all_to_all x1, waiting for transfers between devices, shards(): lax.all_to_all(my_cols.astype(jnp.bfloat16), 'expert', split_axis=0, conc...  5.66 us
    all_to_all x1, starting transfers between devices, shards(): lax.all_to_all(outbound, 'expert', split_axis=0, concat_axis=0, tiled=True)  5.39 us
    all_to_all x1, starting transfers between devices, shards(): lax.all_to_all(my_cols.astype(jnp.bfloat16), 'expert', split_axis=0, conc...  4.59 us
  transfers between devices with their start and end apart: 3, of which 3 were waited for; matrix products, arithmetic and copies ran while one was open for 1% of the time, Pallas kernels for 0%

commit v1 on v0

--- a/solution.py
+++ b/solution.py
@@ -74,7 +74,7 @@
         .reshape(batch_rows, local_heads * head_dim)
     )
     partial_value = jnp.dot(attended, out_proj, preferred_element_type=jnp.float32)
-    attention = lax.psum(partial_value, "group")
+    attention = jnp.sum(lax.all_gather(partial_value, "group"), axis=0)
     hidden = residual.astype(jnp.float32) + attention
     full_rows = lax.all_gather(hidden, "seq", axis=1, tiled=True)
     meansq = jnp.mean(full_rows * full_rows, axis=-1, keepdims=True)

time: 166 us -> 161 us (0.970)
  blocking collectives: 28.9 us -> 24.2 us
    psum x1 -> x0, blocking collectives: 10.3 us -> none  [shards(): attention = lax.psum(partial_value, 'group')]
    all_gather x0 -> x1, blocking collectives: none -> 5.54 us  [shards(): attention = jnp.sum(lax.all_gather(partial_value, 'group'), axis=0)]
where the time goes in v1:
time: 161 us; the launch traced here: 160 us
  waiting for transfers between devices  62.3 us (39%)
  matrix products  40.5 us (25%)
  blocking collectives  24.2 us (15%)
  between operations  13.5 us (8%)
  starting transfers between devices  9.85 us (6%)
  other arithmetic  7.82 us (5%)
  local copies, waits for them, and re-layouts  1.72 us (1%)
    psum x1, waiting for transfers between devices, shards(): lax.psum(down_terms.astype(jnp.bfloat16), ('group', 'seq'))  52.6 us
    dot_general x1, matrix products, shards(): jnp.einsum('secf,efd->secd', activated, w_down, preferred_element_type=jn...  21.8 us
    all_gather x3, blocking collectives, combined_all(): everything = jax.tree.map(lambda part: lax.all_gather(part, axis), value)  14.1 us
    dot_general x1, matrix products, shards(): jnp.einsum('secd,edf->secf', inbound, w_gate, preferred_element_type=jnp....  11.6 us
    all_to_all x1, waiting for transfers between devices, shards(): lax.all_to_all(my_cols.astype(jnp.bfloat16), 'expert', split_axis=0, conc...  5.66 us
    all_gather x1, blocking collectives, shards(): attention = jnp.sum(lax.all_gather(partial_value, 'group'), axis=0)  5.54 us
    all_to_all x1, starting transfers between devices, shards(): lax.all_to_all(outbound, 'expert', split_axis=0, concat_axis=0, tiled=True)  5.25 us
    all_to_all x1, starting transfers between devices, shards(): lax.all_to_all(my_cols.astype(jnp.bfloat16), 'expert', split_axis=0, conc...  4.59 us
  transfers between devices with their start and end apart: 3, of which 3 were waited for; matrix products, arithmetic and copies ran while one was open for 1% of the time, Pallas kernels for 0%

profile of v1, /device:TPU:0, one launch (start us, length us, event | category | flops | bytes accessed | tf_op | source)
XLA Modules:
  0.0 159.9 jit_solution(5313841566095392656)
XLA Ops:
  6.5 0.8 fusion.56
  7.3 0.7 fusion.55
  8.1 0.7 broadcast_multiply_fusion
  9.0 0.7 add_compare_fusion
  9.8 1.0 fusion.64
  10.8 5.3 %all-gather.1 = f32[8,2,4]{2,1,0:T(2,128)S(1)} all-gather(f32[4,2,4]{2,1,0:T(2,128)S(1)} %get-tuple-element.22), channel_id=3, replica_groups=mesh['group'=4,'seq'=2,'expert'=4] {'seq'}, dimensions={0}, use_global_device_ids=true | all-gather | bytes 384 | tf_op jit(solution)/shard_map/all_gather | solution.py:12
  16.1 0.2 fusion.44
  16.3 1.2 fusion.29
  17.4 4.4 %all-gather = f32[8,2,4,128]{3,2,1,0:T(4,128)S(1)} all-gather(f32[4,2,4,128]{3,2,1,0:T(4,128)S(1)} %fusion.29), channel_id=2, replica_groups=mesh['group'=4,'seq'=2,'expert'=4] {'seq'}, dimensions={0}, use_global_device_ids=true | all-gather | bytes 49152 | tf_op jit(solution)/shard_map/all_gather | solution.py:12
  21.8 4.3 %all-gather.2 = f32[8,2,4]{2,1,0:T(2,128)S(1)} all-gather(f32[4,2,4]{2,1,0:T(2,128)S(1)} %fusion.44), channel_id=4, replica_groups=mesh['group'=4,'seq'=2,'expert'=4] {'seq'}, dimensions={0}, use_global_device_ids=true | all-gather | bytes 384 | tf_op jit(solution)/shard_map/all_gather | solution.py:12
  26.2 0.1 fusion.43
  26.3 2.8 %convolution_bitcast_fusion.1 = f32[1,4,2048]{2,1,0:T(4,128)S(1)} fusion(bf16[4,1024]{1,0:T(4,128)(2,1)S(1)} %reshape.186, bf16[1024,2048]{1,0:T(8,128)(2,1)} %param.18), kind=kOutput, calls=%fused_computation.12 | convolution fusion | flops 16777216 | bytes 4235264 | tf_op jit(solution)/shard_map/dot_general | solution.py:76
  29.2 5.5 %all-gather.4 = f32[4,4,2048]{2,1,0:T(4,128)S(1)} all-gather(f32[1,4,2048]{2,1,0:T(4,128)S(1)} %convolution_bitcast_fusion.1), channel_id=5, replica_groups=mesh['group'=4,'seq'=2,'expert'=4] {'group'}, dimensions={0}, use_global_device_ids=true | all-gather | bytes 163840 | tf_op jit(solution)/shard_map/all_gather | solution.py:77
  34.8 0.9 select_reduce_fusion
  35.7 0.7 convert_add_fusion
  36.4 4.6 %all_gather.35 = f32[4,4096]{1,0:T(4,128)S(1)} all-gather(f32[4,2048]{1,0:T(4,128)S(1)} %convert_add_fusion), channel_id=1, replica_groups=mesh['group'=4,'seq'=2,'expert'=4] {'seq'}, dimensions={1}, use_global_device_ids=true | all-gather | bytes 98304 | tf_op jit(solution)/shard_map/all_gather | solution.py:79
  41.0 0.7 convert_element_type.66
  41.7 0.1 multiply_reduce_fusion
  42.0 0.2 convolution_convert_fusion
  42.3 0.8 copy.42
  43.1 5.3 %all-to-all-start = ((bf16[4,2,2,4096]{3,2,1,0:T(2,128)(2,1)}), bf16[4,2,2,4096]{3,2,1,0:T(2,128)(2,1)S(1)}, u32[]{:S(2)}, u32[]{:S(2)}) async-start(bf16[4,2,2,4096]{3,2,1,0:T(2,128)(2,1)} %bitcast.3), calls=%async_computation | async-start | bytes 262144 | tf_op jit(solution)/shard_map/all_to_all | solution.py:106
  48.3 1.0 fusion.65
  49.3 0.9 multiply_reduce_fusion.2
  50.2 4.0 %all-to-all-done = bf16[4,2,2,4096]{3,2,1,0:T(2,128)(2,1)S(1)} async-done(((bf16[4,2,2,4096]{3,2,1,0:T(2,128)(2,1)}), bf16[4,2,2,4096]{3,2,1,0:T(2,128)(2,1)S(1)}, u32[]{:S(2)}, u32[]{:S(2)}) %all-to-all-start) | async-done | bytes 131104 | tf_op jit(solution)/shard_map/all_to_all | solution.py:106
  54.2 11.6 %fusion.12 = f32[4,2,2,1792]{3,0,2,1:T(4,128)S(1)} fusion(bf16[2,4096,1792]{2,1,0:T(8,128)(2,1)} %param.23, bf16[4,2,2,4096]{3,2,1,0:T(2,128)(2,1)S(1)} %all-to-all-done), kind=kOutput, calls=%fused_computation.9 | convolution fusion | flops 234881024 | bytes 29605888 | tf_op jit(solution)/shard_map/secd,edf->secf/dot_general | solution.py:107
  65.8 21.8 %fusion.9 = bf16[4,2,2,4096]{3,0,2,1:T(4,128)(2,1)} fusion(bf16[2,1792,4096]{2,1,0:T(8,128)(2,1)} %param.25, bf16[2,4096,1792]{2,1,0:T(8,128)(2,1)} %param.24, f32[4,2,2,1792]{3,0,2,1:T(4,128)S(1)} %fusion.12, bf16[4,2,2,4096]{3,2,1,0:T(2,128)(2,1)S(1)} %all-to-all-done), kind=kOutput, calls=%fused_computation.8 | convolution fusion | flops 469999616 | bytes 59097088 | tf_op jit(solution)/shard_map/secf,efd->secd/dot_general | solution.py:110
  87.7 52.6 %all-reduce.2.cloned.1.call-done = bf16[4,2,2,4096]{3,0,2,1:T(4,128)(2,1)} async-done(((bf16[4,2,2,4096]{3,0,2,1:T(4,128)(2,1)}), bf16[4,2,2,4096]{3,0,2,1:T(4,128)(2,1)}) %all-reduce.2.cloned.1.call-update) | async-done | bytes 131088 | tf_op jit(solution)/shard_map/psum | solution.py:111
  140.3 0.9 convert_convert_fusion
  141.1 0.7 copy.37
  141.8 4.6 %all-to-all-start.1 = ((bf16[4,2,2,2048]{3,2,1,0:T(2,128)(2,1)}), bf16[4,2,2,2048]{3,2,1,0:T(2,128)(2,1)S(1)}, u32[]{:S(2)}, u32[]{:S(2)}) async-start(bf16[4,2,2,2048]{3,2,1,0:T(2,128)(2,1)} %copy.37), calls=%async_computation.1 | async-start | bytes 131072 | tf_op jit(solution)/shard_map/all_to_all | solution.py:114
  146.5 5.7 %all-to-all-done.1 = bf16[4,2,2,2048]{3,2,1,0:T(2,128)(2,1)S(1)} async-done(((bf16[4,2,2,2048]{3,2,1,0:T(2,128)(2,1)}), bf16[4,2,2,2048]{3,2,1,0:T(2,128)(2,1)S(1)}, u32[]{:S(2)}, u32[]{:S(2)}) %all-to-all-start.1) | async-done | bytes 65568 | tf_op jit(solution)/shard_map/all_to_all | solution.py:114
  152.2 0.8 fusion.27
  (21 shorter events, 0.7 us)
Async XLA Ops:
  6.5 3.2 %copy-start = (bf16[4,128,2,128]{3,2,1,0:T(2,128)(2,1)S(1)}, bf16[4,128,2,128]{3,2,1,0:T(2,128)(2,1)}, u32[]{:S(2)}) copy-start(bf16[4,128,2,128]{3,2,1,0:T(2,128)(2,1)} %param.14) | copy-start | bytes 786436
  43.1 11.2 %all-to-all-start = ((bf16[4,2,2,4096]{3,2,1,0:T(2,128)(2,1)}), bf16[4,2,2,4096]{3,2,1,0:T(2,128)(2,1)S(1)}, u32[]{:S(2)}, u32[]{:S(2)}) async-start(bf16[4,2,2,4096]{3,2,1,0:T(2,128)(2,1)} %bitcast.3), calls=%async_computation | async-start | bytes 262144 | tf_op jit(solution)/shard_map/all_to_all | solution.py:106
  48.3 92.0 %all-reduce.2.cloned.1.call-start = ((), (), s32[]{:S(2)}) async-start(), calls=%async_computation.2 | async-start | bytes 262144 | tf_op jit(solution)/shard_map/psum | solution.py:111
  141.8 10.3 %all-to-all-start.1 = ((bf16[4,2,2,2048]{3,2,1,0:T(2,128)(2,1)}), bf16[4,2,2,2048]{3,2,1,0:T(2,128)(2,1)S(1)}, u32[]{:S(2)}, u32[]{:S(2)}) async-start(bf16[4,2,2,2048]{3,2,1,0:T(2,128)(2,1)} %copy.37), calls=%async_computation.1 | async-start | bytes 131072 | tf_op jit(solution)/shard_map/all_to_all | solution.py:114
Sparse Core Ops, SparseCore 0:
  87.8 52.4 all-reduce.1
